TPU v7x, 32 devices: a whole 2x2x4 slice. The times are simulated.
32 devices in a mesh: gx: 8 (over z, x), gy: 4 (over y, core).
Axes of the slice: x: 2, y: 2, z: 4, core: 2. Of those that a mesh axis runs over, the one named last changes fastest.
Arguments:
- orbitals: bfloat16 [20000, 200], P('gx'), may hold values from -6 to 6
- projector: bfloat16 [6016, 20000], P('gy', 'gx'), may hold values from -0.0390625 to 0.0390625
- integrals: bfloat16 [8, 6016, 6016], P('gx', 'gy'), may hold values from -1 to 1
Outputs:
- exchange_matrix: float32 [6016, 6016], P('gx', 'gy')
- exchange_orbitals: float32 [20000, 200], P('gx', 'gy')
- energy_mean: float32 [], replicated
- trace_mean: float32 [], replicated
All inputs are finite; a program needn't handle non-finite values.
Results may differ from a plain program's by a relative error of at most 0.008.
Values may be sent and summed in bfloat16 or wider, within the bound.
No kernel may reach another device: no remote copies, remote signals or barrier semaphores. Data moves between devices by JAX's collectives and lax.ppermute only.
A program may use at most 128 MiB of HBM per device.

v0:
```python
import jax
import jax.numpy as jnp
from jax import lax
from jax.sharding import PartitionSpec as P


def spread(block, axis, holder):
    block = jnp.where(lax.axis_index(axis) == holder, block, jnp.zeros_like(block))
    return lax.psum(block, axis)


def on_device(orbitals, projector, integrals):
    part_rows = projector.shape[0]
    partial_value = jnp.dot(projector, orbitals, preferred_element_type=jnp.float32)
    own_admm = lax.psum(partial_value, "gx").astype(jnp.bfloat16)
    admm = lax.all_gather(own_admm, "gy", axis=0, tiled=True)
    half = lax.dot_general(
        integrals, admm, (((2,), (0,)), ((), ())), preferred_element_type=jnp.float32
    ).astype(jnp.bfloat16)
    size_x = lax.axis_size("gx")
    block_rows = admm.shape[0] // size_x
    index_x = lax.axis_index("gx")
    index_y = lax.axis_index("gy")
    all_half = lax.all_gather(half, "gx", axis=0, tiled=True)
    first_row = index_x * block_rows
    root = first_row // part_rows
    offset = jnp.clip(first_row - index_y * part_rows, 0, part_rows - block_rows)
    mine = lax.dynamic_slice_in_dim(all_half, offset, block_rows, 1)
    columns = spread(mine, "gy", root)
    exchange = lax.dot_general(
        columns, all_half, (((0, 2), (0, 2)), ((), ())), preferred_element_type=jnp.float32
    )
    row_ids = index_x * block_rows + lax.iota(jnp.int32, block_rows)
    col_ids = index_y * part_rows + lax.iota(jnp.int32, part_rows)
    diag_mask = row_ids[:, None] == col_ids[None, :]
    trace_part = jnp.sum(jnp.where(diag_mask, exchange, 0.0))
    trace_total = lax.psum(trace_part, ("gx", "gy"))
    admm_wide = admm.astype(jnp.float32)
    col_orbs = lax.dynamic_slice_in_dim(admm_wide, index_x * block_rows, block_rows, 0)
    row_orbs = lax.dynamic_slice_in_dim(admm_wide, index_y * part_rows, part_rows, 0)
    applied_part = lax.dot_general(
        exchange,
        col_orbs,
        (((0,), (0,)), ((), ())),
        precision=lax.Precision.HIGHEST,
        preferred_element_type=jnp.float32,
    )
    energy_part = jnp.sum(row_orbs * applied_part)
    energy_total = lax.psum(energy_part, ("gx", "gy"))
    applied = lax.psum(applied_part, "gx")
    applied_low = applied.astype(jnp.bfloat16)
    back_part = lax.dot_general(
        projector, applied_low, (((0,), (0,)), ((), ())), preferred_element_type=jnp.float32
    )
    back = lax.psum_scatter(back_part, "gy", scatter_dimension=1, tiled=True)
    total_adm = admm.shape[0]
    energy_mean = -0.5 * energy_total / (total_adm * admm.shape[1])
    trace_mean = trace_total / total_adm
    return (exchange, back, energy_mean, trace_mean)


def solution(mesh):
    return jax.shard_map(
        on_device,
        mesh=mesh,
        in_specs=(P("gx", None), P("gy", "gx"), P("gx", "gy", None)),
        out_specs=(P("gx", "gy"), P("gx", "gy"), P(), P()),
        check_vma=False,
    )
```

profile of v0, /device:TPU:12, one launch (start us, length us, event | category | flops | bytes accessed | tf_op | source)
XLA Modules:
  0.0 447.2 jit_solution(2069144303628339878)
XLA Ops:
  7.2 0.0 copy-start
  7.2 0.0 all-gather.6.cloned.1.call-start
  7.2 1.2 copy-done
  8.4 4.9 %fusion.13 = f32[1504,200]{0,1:T(8,128)S(1)} fusion(bf16[1504,2500]{0,1:T(8,128)(2,1)} %param.4, bf16[2500,200]{0,1:T(8,128)(2,1)S(1)} %copy-done), kind=kOutput, calls=%fused_computation.17 | convolution fusion | flops 1504000000 | bytes 9723200 | tf_op jit(solution)/shard_map/dot_general | solution.py:14
  13.3 72.9 %all-reduce.8 = bf16[1504,200]{0,1:T(8,128)(2,1)} all-reduce(f32[1504,200]{0,1:T(8,128)S(1)} %fusion.13), channel_id=1, replica_groups=mesh['gx'=8,'gy'=4] {'gx'}, use_global_device_ids=true, to_apply=%region_0.0 | all-reduce | flops 300800 | bytes 1804800 | tf_op jit(solution)/shard_map/psum | solution.py:15
  86.2 0.0 all-gather.6.cloned.1.call-update
  86.2 0.0 all-gather.8.cloned.1.call-start
  86.3 23.8 %all-gather.6.cloned.1.call-done = bf16[4,1504,200]{1,2,0:T(8,128)(2,1)} async-done(((bf16[1,1504,200]{1,2,0:T(8,128)(2,1)}), bf16[4,1504,200]{1,2,0:T(8,128)(2,1)}) %all-gather.6.cloned.1.call-update) | async-done | bytes 2406416 | tf_op jit(solution)/shard_map/all_gather | solution.py:16
  110.1 3.0 copy.8
  113.1 4.4 reshape.24
  117.5 13.3 %fusion.6 = bf16[1,1504,200]{1,2,0:T(8,128)(2,1)} fusion(bf16[6016,200]{0,1:T(8,128)(2,1)} %reshape.24, bf16[1,1504,6016]{2,1,0:T(8,128)(2,1)} %param.5), kind=kOutput, calls=%fused_computation.7 | convolution fusion | flops 3619526400 | bytes 21104128 | tf_op jit(solution)/shard_map/dot_general | solution.py:17
  130.8 0.0 all-gather.8.cloned.1.call-update
  130.8 0.2 all-reduce.7.cloned.1.call-start
  131.1 81.9 %all-gather.8.cloned.1.call-done = bf16[8,1504,200]{1,2,0:T(8,128)(2,1)} async-done(((bf16[1,1504,200]{1,2,0:T(8,128)(2,1)}), bf16[8,1504,200]{1,2,0:T(8,128)(2,1)}) %all-gather.8.cloned.1.call-update) | async-done | bytes 4812816 | tf_op jit(solution)/shard_map/all_gather | solution.py:24
  213.0 4.8 %dynamic-slice_select_fusion = bf16[8,752,200]{1,2,0:T(8,128)(2,1)} fusion(bf16[8,1504,200]{1,2,0:T(8,128)(2,1)} %all-gather.8.cloned.1.call-done, s32[]{:T(128)S(6)} %min.4, pred[]{:T(512)S(6)} %eq.16), kind=kLoop, calls=%fused_computation.6 | loop fusion | flops 1203200 | bytes 4812805 | tf_op jit(solution)/shard_map/jit(_where)/select_n | solution.py:8
  217.8 0.0 all-reduce.7.cloned.1.call-update
  217.9 55.5 %all-reduce.7.cloned.1.call-done = bf16[8,752,200]{1,2,0:T(8,128)(2,1)} async-done(((bf16[8,752,200]{1,2,0:T(8,128)(2,1)}), bf16[8,752,200]{1,2,0:T(8,128)(2,1)}) %all-reduce.7.cloned.1.call-update) | async-done | bytes 2406416 | tf_op jit(solution)/shard_map/psum | solution.py:9
  273.4 8.1 %select_reduce_fusion = (f32[]{:T(128)}, f32[752,1504]{1,0:T(8,128)S(1)}) fusion(s32[1504]{0:T(1024)S(1)} %iota_add_fusion, s32[752]{0:T(1024)S(1)} %iota_add_fusion.1, bf16[8,752,200]{1,2,0:T(8,128)(2,1)} %all-reduce.7.cloned.1.call-done, bf16[8,1504,200]{1,2,0:T(8,128)(2,1)} %all-gather.8.cloned.1.call-done), kind=kOutput, calls=%fused_computation.2 | convolution fusion | flops 3622618624 | bytes 11752260 | tf_op jit(solution)/shard_map/dot_general | solution.py:30
  281.5 0.0 copy-start.1
  281.5 5.0 %multiply_reduce_fusion = (f32[]{:T(128)}, f32[1504,200]{0,1:T(8,128)S(1)}) fusion(bf16[6016,200]{0,1:T(8,128)(2,1)} %reshape.24, s32[]{:T(128)S(6)} %select_n.28, f32[752,1504]{1,0:T(8,128)S(1)} %get-tuple-element.9, s32[]{:T(128)S(6)} %select_n.27), kind=kOutput, calls=%fused_computation.8 | convolution fusion | flops 2715321600 | bytes 6648844 | tf_op jit(solution)/shard_map/dot_general | solution.py:41
  286.6 0.0 copy-done.1
  286.6 72.6 %all-reduce.9 = bf16[1504,200]{0,1:T(8,128)(2,1)S(1)} all-reduce(f32[1504,200]{0,1:T(8,128)S(1)} %get-tuple-element.7), channel_id=1, replica_groups=mesh['gx'=8,'gy'=4] {'gx'}, use_global_device_ids=true, to_apply=%region_2.3 | all-reduce | flops 300800 | bytes 1804800 | tf_op jit(solution)/shard_map/psum | solution.py:50
  359.2 7.0 %convolution_bitcast_fusion = f32[2500,200]{0,1:T(8,128)} fusion(bf16[1504,2500]{0,1:T(8,128)(2,1)} %param.4, bf16[1504,200]{0,1:T(8,128)(2,1)S(1)} %all-reduce.9), kind=kOutput, calls=%fused_computation.3 | convolution fusion | flops 1504000000 | bytes 10121600 | tf_op jit(solution)/shard_map/dot_general | solution.py:52
  366.1 0.0 copy-start.2
  366.1 24.2 %fusion = f32[2500,56]{0,1:T(8,128)S(1)} fusion(f32[2500,200]{0,1:T(8,128)} %convolution_bitcast_fusion), kind=kCustom, calls=%all-reduce-scatter | all-reduce-scatter fusion | flops 560001 | bytes 2560512
  390.3 1.9 collective-permute-start
  392.2 0.0 copy-done.2
  392.3 0.6 dynamic-slice.5
  393.5 42.3 %all-reduce.2 = (f32[]{:T(128)}, f32[]{:T(128)}) all-reduce(f32[]{:T(128)} %get-tuple-element.6, f32[]{:T(128)} %get-tuple-element.8), channel_id=1, replica_groups=mesh['gx'=8,'gy'=4] {'gx','gy'}, use_global_device_ids=true, to_apply=%region_5.6 | all-reduce | flops 2 | bytes 16 | tf_op jit(solution)/shard_map/psum | solution.py:49
  437.1 0.0 collective-permute-done
  437.1 0.4 concatenate
  437.6 0.9 constant_dynamic-slice_fusion
  (3 shorter events, 0.0 us)
Async XLA Ops:
  7.2 1.2 copy-start
  7.2 102.9 %all-gather.6.cloned.1.call-start = ((), (), s32[]{:S(2)}) async-start(), calls=%async_computation.1 | async-start | bytes 3072000 | tf_op jit(solution)/shard_map/all_gather | solution.py:16
  86.2 126.8 %all-gather.8.cloned.1.call-start = ((), (), s32[]{:S(2)}) async-start(), calls=%async_computation.2 | async-start | bytes 5529600 | tf_op jit(solution)/shard_map/all_gather | solution.py:24
  130.8 142.6 %all-reduce.7.cloned.1.call-start = ((), (), s32[]{:S(2)}) async-start(), calls=%async_computation | async-start | bytes 4915200 | tf_op jit(solution)/shard_map/psum | solution.py:9
  281.5 5.0 %copy-start.1 = (f32[752,1504]{1,0:T(8,128)}, f32[752,1504]{1,0:T(8,128)S(1)}, u32[]{:S(2)}) copy-start(f32[752,1504]{1,0:T(8,128)S(1)} %get-tuple-element.9) | copy-start | bytes 13572100
  366.1 26.1 %copy-start.2 = (u32[32]{0:T(128)S(1)}, u32[32]{0:T(128)}, u32[]{:S(2)}) copy-start(u32[32]{0:T(128)} %constant.44) | copy-start | bytes 388
  390.3 46.8 %collective-permute-start = (f32[2500,18]{0,1:T(8,128)S(1)}, f32[2500,18]{0,1:T(8,128)S(1)}, u32[]{:S(2)}, u32[]{:S(2)}) collective-permute-start(f32[2500,18]{0,1:T(8,128)S(1)} %slice), channel_id=1, source_target_pairs={{0,1},{1,2},{2,3},{4,5},{5,6},{6,7},{8,9},{9,10},{10,11},{12,13},{... | collective-permute-start | bytes 540008
Sparse Core Ops, SparseCore 0:
  86.3 23.7 all-gather.5
  130.9 82.0 all-gather.7
  218.0 55.3 all-reduce.6
where the time goes:
time: 448 us; the launch traced here: 447 us
  blocking collectives  212 us (47%)
  waiting for transfers between devices  161 us (36%)
  matrix products  38.4 us (9%)
  between operations  18.1 us (4%)
  local copies, waits for them, and re-layouts  10.4 us (2%)
  other arithmetic  4.83 us (1%)
    all_gather x1, waiting for transfers between devices, on_device(): all_half = lax.all_gather(half, 'gx', axis=0, tiled=True)  81.9 us
    psum x1, blocking collectives, on_device(): own_admm = lax.psum(partial_value, 'gx').astype(jnp.bfloat16)  72.9 us
    psum x1, blocking collectives, on_device(): applied = lax.psum(applied_part, 'gx')  72.6 us
    psum x1, waiting for transfers between devices, spread(): return lax.psum(block, axis)  55.5 us
    psum x1, blocking collectives, on_device(): energy_total = lax.psum(energy_part, ('gx', 'gy'))  42.3 us
    unnamed x1, blocking collectives  24.2 us
    all_gather x1, waiting for transfers between devices, on_device(): admm = lax.all_gather(own_admm, 'gy', axis=0, tiled=True)  23.8 us
    dot_general x1, matrix products, on_device(): lax.dot_general(integrals, admm, (((2,), (0,)), ((), ())), preferred_elem...  13.3 us
  transfers between devices with their start and end apart: 4, of which 3 were waited for; matrix products, arithmetic and copies ran while one was open for 0% of the time, Pallas kernels for 0%

commit v1 on v0

--- a/solution.py
+++ b/solution.py
@@ -47,7 +47,10 @@
     )
     energy_part = jnp.sum(row_orbs * applied_part)
     energy_total = lax.psum(energy_part, ("gx", "gy"))
-    applied = lax.psum(applied_part, "gx")
+    size, applied = (lax.axis_size("gx"), applied_part)
+    for hop in [1 << k for k in range(size.bit_length() - 1)]:
+        route = [(i, i ^ hop) for i in range(size)]
+        applied = applied + lax.ppermute(applied, "gx", route)
     applied_low = applied.astype(jnp.bfloat16)
     back_part = lax.dot_general(
         projector, applied_low, (((0,), (0,)), ((), ())), preferred_element_type=jnp.float32

time: 448 us -> 488 us (1.089)
  waiting for transfers between devices: 161 us -> 267 us
  blocking collectives: 212 us -> 140 us
    ppermute x0 -> x3, waiting for transfers between devices: none -> 105 us  [on_device(): applied = applied + lax.ppermute(applied, 'gx', route)]
    psum x1 -> x0, blocking collectives: 72.6 us -> none  [on_device(): applied = lax.psum(applied_part, 'gx')]
  transfers between devices with their start and end apart: 4 -> 7, of which waited for: 3 -> 6; matrix products, arithmetic and copies ran while one was open for 0% -> 0% of each run, Pallas kernels for 0% -> 0%
where the time goes in v1:
time: 488 us; the launch traced here: 487 us
  waiting for transfers between devices  267 us (55%)
  blocking collectives  140 us (29%)
  matrix products  35.5 us (7%)
  between operations  18.1 us (4%)
  local copies, waits for them, and re-layouts  13.1 us (3%)
  other arithmetic  7.16 us (1%)
  starting transfers between devices  6.74 us (1%)
    ppermute x3, waiting for transfers between devices, on_device(): applied = applied + lax.ppermute(applied, 'gx', route)  105 us
    all_gather x1, waiting for transfers between devices, on_device(): all_half = lax.all_gather(half, 'gx', axis=0, tiled=True)  81.9 us
    psum x1, blocking collectives, on_device(): own_admm = lax.psum(partial_value, 'gx').astype(jnp.bfloat16)  72.9 us
    psum x1, waiting for transfers between devices, spread(): return lax.psum(block, axis)  55.5 us
    psum x1, blocking collectives, on_device(): energy_total = lax.psum(energy_part, ('gx', 'gy'))  42.4 us
    unnamed x1, blocking collectives  24.8 us
    all_gather x1, waiting for transfers between devices, on_device(): admm = lax.all_gather(own_admm, 'gy', axis=0, tiled=True)  23.8 us
    dot_general x1, matrix products, on_device(): lax.dot_general(integrals, admm, (((2,), (0,)), ((), ())), preferred_elem...  13.3 us
  transfers between devices with their start and end apart: 7, of which 6 were waited for; matrix products, arithmetic and copies ran while one was open for 0% of the time, Pallas kernels for 0%

profile of v1, /device:TPU:12, one launch (start us, length us, event | category | flops | bytes accessed | tf_op | source)
XLA Modules:
  0.0 487.2 jit_solution(8584397555581029447)
XLA Ops:
  7.2 0.0 all-gather.6.cloned.1.call-start
  7.2 1.2 copy-done
  8.4 4.9 %fusion.12 = f32[1504,200]{0,1:T(8,128)S(1)} fusion(bf16[1504,2500]{0,1:T(8,128)(2,1)} %param.4, bf16[2500,200]{0,1:T(8,128)(2,1)S(1)} %copy-done), kind=kOutput, calls=%fused_computation.17 | convolution fusion | flops 1504000000 | bytes 9723200 | tf_op jit(solution)/shard_map/dot_general | solution.py:14
  13.3 72.9 %all-reduce.7 = bf16[1504,200]{0,1:T(8,128)(2,1)} all-reduce(f32[1504,200]{0,1:T(8,128)S(1)} %fusion.12), channel_id=1, replica_groups=mesh['gx'=8,'gy'=4] {'gx'}, use_global_device_ids=true, to_apply=%region_0.0 | all-reduce | flops 300800 | bytes 1804800 | tf_op jit(solution)/shard_map/psum | solution.py:15
  86.2 0.0 all-gather.6.cloned.1.call-update
  86.2 0.0 all-gather.8.cloned.1.call-start
  86.3 23.8 %all-gather.6.cloned.1.call-done = bf16[4,1504,200]{1,2,0:T(8,128)(2,1)} async-done(((bf16[1,1504,200]{1,2,0:T(8,128)(2,1)}), bf16[4,1504,200]{1,2,0:T(8,128)(2,1)}) %all-gather.6.cloned.1.call-update) | async-done | bytes 2406416 | tf_op jit(solution)/shard_map/all_gather | solution.py:16
  110.1 3.0 copy.8
  113.1 4.4 reshape.24
  117.5 13.3 %fusion.6 = bf16[1,1504,200]{1,2,0:T(8,128)(2,1)} fusion(bf16[6016,200]{0,1:T(8,128)(2,1)} %reshape.24, bf16[1,1504,6016]{2,1,0:T(8,128)(2,1)} %param.5), kind=kOutput, calls=%fused_computation.7 | convolution fusion | flops 3619526400 | bytes 21104128 | tf_op jit(solution)/shard_map/dot_general | solution.py:17
  130.8 0.2 all-reduce.6.cloned.1.call-start
  131.1 81.9 %all-gather.8.cloned.1.call-done = bf16[8,1504,200]{1,2,0:T(8,128)(2,1)} async-done(((bf16[1,1504,200]{1,2,0:T(8,128)(2,1)}), bf16[8,1504,200]{1,2,0:T(8,128)(2,1)}) %all-gather.8.cloned.1.call-update) | async-done | bytes 4812816 | tf_op jit(solution)/shard_map/all_gather | solution.py:24
  213.0 4.8 dynamic-slice_select_fusion
  217.8 55.5 %all-reduce.6.cloned.1.call-done = bf16[8,752,200]{1,2,0:T(8,128)(2,1)} async-done(((bf16[8,752,200]{1,2,0:T(8,128)(2,1)}), bf16[8,752,200]{1,2,0:T(8,128)(2,1)}) %all-reduce.6.cloned.1.call-update) | async-done | bytes 2406416 | tf_op jit(solution)/shard_map/psum | solution.py:9
  273.4 8.1 %select_reduce_fusion = (f32[]{:T(128)}, f32[752,1504]{1,0:T(8,128)S(1)}) fusion(s32[1504]{0:T(1024)S(1)} %iota_add_fusion, s32[752]{0:T(1024)S(1)} %iota_add_fusion.1, bf16[8,752,200]{1,2,0:T(8,128)(2,1)} %all-reduce.6.cloned.1.call-done, bf16[8,1504,200]{1,2,0:T(8,128)(2,1)} %all-gather.8.cloned.1.call-done), kind=kOutput, calls=%fused_computation.2 | convolution fusion | flops 3622618624 | bytes 11752260 | tf_op jit(solution)/shard_map/dot_general | solution.py:30
  281.5 3.4 fusion.9
  285.0 1.5 collective-permute-start
  286.5 27.2 %collective-permute-done = f32[1504,200]{0,1:T(8,128)S(1)} collective-permute-done((f32[1504,200]{0,1:T(8,128)S(1)}, f32[1504,200]{0,1:T(8,128)S(1)}, u32[]{:S(2)}, u32[]{:S(2)}) %collective-permute-start) | collective-permute-done | bytes 1203232 | tf_op jit(solution)/shard_map/ppermute | solution.py:53
  313.7 2.2 multiply_reduce_fusion
  315.9 0.5 collective-permute-start.1
  316.4 27.3 %collective-permute-done.1 = f32[1504,200]{0,1:T(8,128)S(1)} collective-permute-done((f32[1504,200]{0,1:T(8,128)S(1)}, f32[1504,200]{0,1:T(8,128)S(1)}, u32[]{:S(2)}, u32[]{:S(2)}) %collective-permute-start.1) | collective-permute-done | bytes 1203232 | tf_op jit(solution)/shard_map/ppermute | solution.py:53
  343.7 0.1 add.49
  343.8 2.5 collective-permute-start.2
  346.3 50.8 %collective-permute-done.2 = f32[1504,200]{0,1:T(8,128)S(1)} collective-permute-done((f32[1504,200]{0,1:T(8,128)S(1)}, f32[1504,200]{0,1:T(8,128)S(1)}, u32[]{:S(2)}, u32[]{:S(2)}) %collective-permute-start.2) | collective-permute-done | bytes 1203232 | tf_op jit(solution)/shard_map/ppermute | solution.py:53
  397.1 5.7 %convolution_bitcast_fusion = f32[2500,200]{0,1:T(8,128)S(1)} fusion(bf16[1504,2500]{0,1:T(8,128)(2,1)} %param.4, f32[1504,200]{0,1:T(8,128)S(1)} %add.49, f32[1504,200]{0,1:T(8,128)S(1)} %collective-permute-done.2), kind=kOutput, calls=%fused_computation.3 | convolution fusion | flops 1504601600 | bytes 11926400 | tf_op jit(solution)/shard_map/dot_general | solution.py:55
  402.8 24.8 %fusion = f32[2500,56]{0,1:T(8,128)} fusion(f32[2500,200]{0,1:T(8,128)S(1)} %convolution_bitcast_fusion), kind=kCustom, calls=%all-reduce-scatter | all-reduce-scatter fusion | flops 560001 | bytes 2560512
  427.6 1.0 slice
  428.5 1.9 collective-permute-start.3
  430.5 0.6 dynamic-slice.5
  431.7 42.4 %all-reduce.2 = (f32[]{:T(128)}, f32[]{:T(128)}) all-reduce(f32[]{:T(128)} %get-tuple-element.6, f32[]{:T(128)} %get-tuple-element.8), channel_id=1, replica_groups=mesh['gx'=8,'gy'=4] {'gx','gy'}, use_global_device_ids=true, to_apply=%region_4.5 | all-reduce | flops 2 | bytes 16 | tf_op jit(solution)/shard_map/psum | solution.py:49
  475.5 2.1 concatenate
  477.5 0.9 constant_dynamic-slice_fusion
  (10 shorter events, 0.1 us)
Async XLA Ops:
  7.2 1.2 copy-start
  7.2 102.9 %all-gather.6.cloned.1.call-start = ((), (), s32[]{:S(2)}) async-start(), calls=%async_computation.1 | async-start | bytes 3072000 | tf_op jit(solution)/shard_map/all_gather | solution.py:16
  86.2 126.8 %all-gather.8.cloned.1.call-start = ((), (), s32[]{:S(2)}) async-start(), calls=%async_computation.2 | async-start | bytes 5529600 | tf_op jit(solution)/shard_map/all_gather | solution.py:24
  130.8 142.6 %all-reduce.6.cloned.1.call-start = ((), (), s32[]{:S(2)}) async-start(), calls=%async_computation | async-start | bytes 4915200 | tf_op jit(solution)/shard_map/psum | solution.py:9
  281.5 3.4 copy-start.1
  285.0 28.8 %collective-permute-start = (f32[1504,200]{0,1:T(8,128)S(1)}, f32[1504,200]{0,1:T(8,128)S(1)}, u32[]{:S(2)}, u32[]{:S(2)}) collective-permute-start(f32[1504,200]{0,1:T(8,128)S(1)} %fusion.9), channel_id=1, source_target_pairs={{0,4},{4,0},{8,12},{12,8},{16,20},{20,16},{24,28},{28,24},{1,5},{5... | collective-permute-start | bytes 3609608 | tf_op jit(solution)/shard_map/ppermute | solution.py:53
  315.9 27.8 %collective-permute-start.1 = (f32[1504,200]{0,1:T(8,128)S(1)}, f32[1504,200]{0,1:T(8,128)S(1)}, u32[]{:S(2)}, u32[]{:S(2)}) collective-permute-start(f32[1504,200]{0,1:T(8,128)S(1)} %get-tuple-element.7), channel_id=1, source_target_pairs={{0,8},{4,12},{8,0},{12,4},{16,24},{20,28},{24,16},{28,20},{1,9},{5... | collective-permute-start | bytes 3609608 | tf_op jit(solution)/shard_map/ppermute | solution.py:53
  343.8 53.3 %collective-permute-start.2 = (f32[1504,200]{0,1:T(8,128)S(1)}, f32[1504,200]{0,1:T(8,128)S(1)}, u32[]{:S(2)}, u32[]{:S(2)}) collective-permute-start(f32[1504,200]{0,1:T(8,128)S(1)} %add.49), channel_id=1, source_target_pairs={{0,16},{4,20},{8,24},{12,28},{16,0},{20,4},{24,8},{28,12},{1,17},{... | collective-permute-start | bytes 3609608 | tf_op jit(solution)/shard_map/ppermute | solution.py:53
  402.8 27.7 %copy-start.2 = (u32[32]{0:T(128)S(1)}, u32[32]{0:T(128)}, u32[]{:S(2)}) copy-start(u32[32]{0:T(128)} %constant.44) | copy-start | bytes 388
  428.5 46.9 %collective-permute-start.3 = (f32[2500,18]{0,1:T(8,128)S(1)}, f32[2500,18]{0,1:T(8,128)S(1)}, u32[]{:S(2)}, u32[]{:S(2)}) collective-permute-start(f32[2500,18]{0,1:T(8,128)S(1)} %slice), channel_id=1, source_target_pairs={{0,1},{1,2},{2,3},{4,5},{5,6},{6,7},{8,9},{9,10},{10,11},{12,13},{... | collective-permute-start | bytes 540008
Sparse Core Ops, SparseCore 0:
  86.3 23.7 all-gather.5
  130.9 82.0 all-gather.7
  217.9 55.3 all-reduce.5
